TPU v7x, 32 devices: a whole 2x2x4 slice. The times are simulated.
32 devices in a mesh: rows: 8 (over z, y), grp: 4 (over x, core).
Axes of the slice: x: 2, y: 2, z: 4, core: 2. Of those that a mesh axis runs over, the one named last changes fastest.
Arguments:
- owner: int32 [1024, 24, 3], P('rows', 'grp'), may hold values from 0 to 7, as said below
- offset: int32 [1024, 24, 3], P('rows', 'grp'), may hold values from 0 to 511
- tables: float32 [12, 4096, 128], P('grp', 'rows'), may hold values from -6 to 6
- w_first: bfloat16 [3072, 1024], P('grp'), may hold values from -0.109375 to 0.109375
- b_first: float32 [1024], replicated, may hold values from -3 to 3
- w_out: float32 [1024], replicated, may hold values from -0.1875 to 0.1875
- labels: int32 [1024], P('rows'), may hold values 0 or 1
Outputs:
- table_grad: float32 [12, 4096, 128], P('grp', 'rows')
- losses: float32 [1024], P(('rows', 'grp'))
Inputs may be any that keep to these rules, and one draw needn't show every extreme that they name: Of the lookups of one device (its 128 samples and 6 features, all three hashes) at most 1032 name one owner, and in every draw some owner gets exactly 1032. Among the lookups of one device to one owner for one table, at most 114 distinct offsets occur, and that bound is reached in every draw.
All inputs are finite; a program needn't handle non-finite values. No bound on the sum of `labels` on one device may be relied on, other than what follows from the above.
Results may differ from a plain program's by a relative error of at most 0.005.
Values may be sent and summed in bfloat16 or wider, within the bound.
A program may use at most 64 MiB of HBM per device.

v0:
```python
import jax
import jax.numpy as jnp
from jax import lax
from jax.sharding import PartitionSpec as P


def head_loss(pre_act, w_out, targets):
    gate_sig = jax.nn.sigmoid(pre_act)
    logits = jnp.sum(pre_act * gate_sig * w_out, axis=1)
    losses = jax.nn.softplus(logits) - targets * logits
    grad_logit = jax.nn.sigmoid(logits) - targets
    grad_pre = (
        grad_logit[:, None] * w_out * (gate_sig * (1.0 + pre_act * (1.0 - gate_sig)))
    ).astype(jnp.bfloat16)
    return (losses, grad_pre)


def run_starts(sorted_values, values_index):
    is_first = jnp.concatenate([jnp.ones((1,), bool), sorted_values[1:] != sorted_values[:-1]])
    return lax.cummax(jnp.where(is_first, values_index, 0), axis=0)


def body(owner, offset, tables, w_first, b_first, w_out, labels):
    row_devices = lax.axis_size("rows")
    bdev_rows, fgrp_count = (owner.shape[0], owner.shape[1])
    rows_dev, emb_width = (tables.shape[1], tables.shape[2])
    lookups = bdev_rows * fgrp_count * 3
    hot_count = 8 * (bdev_rows * fgrp_count * 7 // (16 * row_devices)) + 8
    owner_flat = owner.reshape(-1)
    offset_flat = offset.reshape(-1)
    positions = jnp.arange(lookups, dtype=jnp.int32)
    table_kind = positions % 3
    flat_table = tables.reshape(3 * rows_dev, emb_width)
    unique_cap = hot_count // 3
    group_key = (owner_flat * 3 + table_kind) * rows_dev + offset_flat
    ordering = jnp.argsort(group_key, stable=True)
    sorted_keys = group_key[ordering]
    is_new = jnp.concatenate([jnp.ones((1,), bool), sorted_keys[1:] != sorted_keys[:-1]])
    unique_id = jnp.cumsum(is_new.astype(jnp.int32)) - 1
    sorted_group = sorted_keys // rows_dev
    slot_sorted = sorted_group * unique_cap + unique_id - run_starts(sorted_group, unique_id)
    slot_of = jnp.zeros((lookups,), jnp.int32).at[ordering].set(slot_sorted)
    outgoing = jnp.full((row_devices * 3 * unique_cap,), -1, jnp.int32).at[slot_of].set(offset_flat)
    row_codes = lax.all_to_all(
        outgoing.reshape(row_devices, 3, unique_cap),
        "rows",
        split_axis=0,
        concat_axis=0,
        tiled=True,
    )
    is_live = (row_codes >= 0)[..., None]
    row_index = jnp.arange(3, dtype=jnp.int32)[None, :, None] * rows_dev + jnp.maximum(row_codes, 0)
    fetched = jnp.take(flat_table, row_index.reshape(-1), axis=0)
    fetched = (fetched.reshape(row_codes.shape + (emb_width,)) * is_live).astype(jnp.bfloat16)
    returned = lax.all_to_all(fetched, "rows", split_axis=0, concat_axis=0, tiled=True)
    owner_codes, returned = (row_codes, returned)
    owner_index = (
        jnp.arange(3, dtype=jnp.int32)[None, :, None] * rows_dev + jnp.maximum(owner_codes, 0)
    ).reshape(-1)
    looked = (
        returned.reshape(-1, emb_width)[slot_of]
        .astype(jnp.float32)
        .reshape(bdev_rows, fgrp_count, 3, emb_width)
    )
    embedded = looked[:, :, 0] * looked[:, :, 1] + looked[:, :, 2]
    features = embedded.reshape(bdev_rows, fgrp_count * emb_width).astype(jnp.bfloat16)
    targets = labels.astype(jnp.float32)
    share_rows = bdev_rows // lax.axis_size("grp")
    share_start = lax.axis_index("grp") * share_rows
    partial_pre = jnp.dot(features, w_first, preferred_element_type=jnp.float32)
    pre_act = lax.psum(partial_pre, "grp") + b_first
    all_losses, grad_pre = head_loss(pre_act, w_out, targets)
    losses = lax.dynamic_slice_in_dim(all_losses, share_start, share_rows, 0)
    grad_emb = jnp.dot(grad_pre, w_first.T, preferred_element_type=jnp.float32).reshape(
        bdev_rows, fgrp_count, emb_width
    )
    row_grads = jnp.stack(
        [grad_emb * looked[:, :, 1], grad_emb * looked[:, :, 0], grad_emb], axis=2
    ).reshape(lookups, emb_width)
    outgoing_grads = (
        jnp.zeros((row_devices * 3 * unique_cap, emb_width), jnp.float32).at[slot_of].add(row_grads)
    )
    received = lax.all_to_all(
        outgoing_grads.reshape(row_devices, 3, unique_cap, emb_width),
        "rows",
        split_axis=0,
        concat_axis=0,
        tiled=True,
    )
    table_grad = (
        jnp.zeros((3 * rows_dev, emb_width), jnp.float32)
        .at[owner_index]
        .add(received.reshape(-1, emb_width))
    )
    return (table_grad.reshape(3, rows_dev, emb_width), losses)


def solution(mesh):
    placed = (
        P("rows", "grp", None),
        P("rows", "grp", None),
        P("grp", "rows", None),
        P("grp", None),
        P(),
        P(),
        P("rows"),
    )
    return jax.shard_map(
        body,
        mesh=mesh,
        in_specs=placed,
        out_specs=(P("grp", "rows", None), P(("rows", "grp"))),
        check_vma=False,
    )
```

profile of v0, /device:TPU:0, one launch (start us, length us, event | category | flops | bytes accessed | tf_op | source)
XLA Modules:
  0.0 225.6 jit_solution(1120389095388177979)
XLA Ops:
  7.2 0.8 broadcast_multiply_fusion
  8.0 0.3 copy.19
  8.3 0.2 mul.93
  8.5 1.0 copy.20
  9.4 0.2 reshape.183
  9.7 5.8 %sort.17 = (s32[2304]{0:T(1024)}, s32[2304]{0:T(1024)S(1)}) sort(s32[2304]{0:T(1024)S(1)} %fusion.12, s32[2304]{0:T(1024)S(1)} %iota.15), dimensions={0}, to_apply=%region_0.1 | sort | flops 27648 | bytes 36864 | tf_op jit(solution)/shard_map/jit(argsort)/sort | solution.py:36
  15.5 12.3 %gather_fusion = s32[2304]{0:T(1024)S(1)} fusion(s32[2304]{0:T(1024)S(1)} %fusion.12, s32[3072]{0:T(1024)S(1)} %pad_clamp_fusion.2), kind=kCustom, calls=%fused_computation | custom fusion | bytes 27648 | tf_op jit(solution)/shard_map/gather | solution.py:37
  27.9 0.3 reduce-window.16
  28.3 0.1 slice_reduce_fusion.1
  28.5 0.1 fusion.19
  28.6 0.3 reduce-window.24
  29.0 0.1 slice_reduce_fusion
  29.1 0.1 bitcast_subtract_fusion
  29.2 9.0 %scatter_custom_fusion = s32[2304]{0:T(1024)S(1)} fusion(s32[2304]{0:T(1024)S(1)} %compare_select_fusion.3, s32[2304]{0:T(1024)S(1)} %bitcast_subtract_fusion, s32[]{:T(128)} %constant.33.clone.1), kind=kCustom, calls=%fused_computation.64 | custom fusion | bytes 9220 | tf_op jit(solution)/shard_map/scatter | solution.py:42
  38.2 9.0 %scatter_custom_fusion.1 = s32[2736]{0:T(1024)S(1)} fusion(s32[2304]{0:T(1024)S(1)} %compare_select_fusion.2, s32[2304]{0:T(1024)S(1)} %reshape.183, s32[]{:T(128)} %constant.31.clone.1), kind=kCustom, calls=%fused_computation.66 | custom fusion | bytes 10948 | tf_op jit(solution)/shard_map/scatter | solution.py:43
  47.3 0.7 reshape.136
  48.0 7.3 %all-to-all-start = ((s32[8,3,114]{2,1,0:T(4,128)}), s32[8,3,114]{2,1,0:T(4,128)S(1)}, u32[]{:S(2)}, u32[]{:S(2)}) async-start(s32[8,3,114]{2,1,0:T(4,128)} %reshape.136), calls=%async_computation | async-start | bytes 32768 | tf_op jit(solution)/shard_map/all_to_all | solution.py:44
  55.3 6.6 %all-to-all-done = s32[8,3,114]{2,1,0:T(4,128)S(1)} async-done(((s32[8,3,114]{2,1,0:T(4,128)}), s32[8,3,114]{2,1,0:T(4,128)S(1)}, u32[]{:S(2)}, u32[]{:S(2)}) %all-to-all-start) | async-done | bytes 10976 | tf_op jit(solution)/shard_map/all_to_all | solution.py:44
  61.8 0.1 compare_and_fusion
  61.9 0.1 reshape.137
  62.1 5.9 %gather_fusion.1 = f32[2736,128]{1,0:T(8,128)} fusion(f32[1536,128]{1,0:T(8,128)S(1)} %bitcast.21, s32[3072]{0:T(1024)S(1)} %pad_clamp_fusion.1), kind=kCustom, calls=%fused_computation.1 | custom fusion | bytes 2812608 | tf_op jit(solution)/shard_map/jit(_take)/gather | solution.py:53
  68.0 1.4 gather.14
  69.5 2.1 multiply_convert_fusion
  71.5 3.5 %all-to-all-start.1 = ((bf16[8,3,114,128]{3,2,1,0:T(8,128)(2,1)}), bf16[8,3,114,128]{3,2,1,0:T(8,128)(2,1)S(1)}, u32[]{:S(2)}, u32[]{:S(2)}) async-start(bf16[8,3,114,128]{3,2,1,0:T(8,128)(2,1)} %multiply_convert_fusion), calls=%async_computation.1 | async-start | bytes 1474560 | tf_op jit(solution)/shard_map/all_to_all | solution.py:55
  75.1 0.2 all-reduce.2.cloned.1.call-start
  75.3 17.6 %all-to-all-done.1 = bf16[8,3,114,128]{3,2,1,0:T(8,128)(2,1)S(1)} async-done(((bf16[8,3,114,128]{3,2,1,0:T(8,128)(2,1)}), bf16[8,3,114,128]{3,2,1,0:T(8,128)(2,1)S(1)}, u32[]{:S(2)}, u32[]{:S(2)}) %all-to-all-start.1) | async-done | bytes 700448 | tf_op jit(solution)/shard_map/all_to_all | solution.py:55
  93.0 0.2 reshape.139
  93.2 5.6 %gather_fusion.2 = bf16[2304,128]{1,0:T(8,128)(2,1)} fusion(bf16[2736,128]{1,0:T(8,128)(2,1)S(1)} %reshape.139, s32[3072]{0:T(1024)S(1)} %pad_clamp_fusion), kind=kCustom, calls=%fused_computation.2 | custom fusion | bytes 1188864 | tf_op jit(solution)/shard_map/gather | solution.py:61
  98.8 2.0 reshape.146
  100.8 0.8 fusion.27
  101.6 0.7 copy-done.2
  102.4 0.1 fusion.2
  102.4 0.2 copy.24
  102.7 1.2 fusion.28
  103.9 32.6 %all-reduce.2.cloned.1.call-done = f32[128,1024]{1,0:T(8,128)} async-done(((f32[128,1024]{1,0:T(8,128)}), f32[128,1024]{1,0:T(8,128)}) %all-reduce.2.cloned.1.call-update) | async-done | bytes 524304 | tf_op jit(solution)/shard_map/psum | solution.py:71
  136.5 1.3 multiply_reduce_fusion
  137.8 1.8 fusion.5
  139.6 0.2 copy.26
  139.9 0.1 pad_maximum_fusion
  139.9 0.8 copy.29
  140.8 1.4 reshape.191
  142.1 14.9 %scatter_custom_fusion.2 = f32[2736,128]{1,0:T(8,128)S(1)} fusion(s32[2304]{0:T(1024)} %copy-done.4, f32[2304,128]{1,0:T(8,128)} %reshape.191, f32[]{:T(128)} %constant.26.clone.1), kind=kCustom, calls=%fused_computation.9 | custom fusion | flops 294912 | bytes 1401344 | tf_op jit(solution)/shard_map/scatter-add | solution.py:81
  157.1 1.2 reshape.142
  158.3 5.5 %all-to-all-start.2 = ((f32[8,3,114,128]{3,2,1,0:T(8,128)}), f32[8,3,114,128]{3,2,1,0:T(8,128)S(1)}, u32[]{:S(2)}, u32[]{:S(2)}) async-start(f32[8,3,114,128]{3,2,1,0:T(8,128)} %reshape.142), calls=%async_computation.2 | async-start | bytes 2949120 | tf_op jit(solution)/shard_map/all_to_all | solution.py:83
  163.8 0.6 dynamic_slice.3
  164.4 33.5 %all-to-all-done.2 = f32[8,3,114,128]{3,2,1,0:T(8,128)S(1)} async-done(((f32[8,3,114,128]{3,2,1,0:T(8,128)}), f32[8,3,114,128]{3,2,1,0:T(8,128)S(1)}, u32[]{:S(2)}, u32[]{:S(2)}) %all-to-all-start.2) | async-done | bytes 1400864 | tf_op jit(solution)/shard_map/all_to_all | solution.py:83
  197.9 1.2 reshape.199
  199.1 19.7 %scatter_custom_fusion.3 = f32[1536,128]{1,0:T(8,128)} fusion(s32[2736]{0:T(1024)S(1)} %fusion.20, f32[2736,128]{1,0:T(8,128)} %reshape.199, f32[]{:T(128)} %constant.26.clone.1), kind=kCustom, calls=%fused_computation.16 | custom fusion | flops 350208 | bytes 786944 | tf_op jit(solution)/shard_map/scatter-add | solution.py:93
  (35 shorter events, 0.7 us)
Async XLA Ops:
  7.2 95.5 %copy-start = (bf16[768,1024]{1,0:T(8,128)(2,1)S(1)}, bf16[768,1024]{1,0:T(8,128)(2,1)}, u32[]{:S(2)}) copy-start(bf16[768,1024]{1,0:T(8,128)(2,1)} %param.10) | copy-start | bytes 4718596
  15.4 46.7 %copy-start.1 = (f32[3,512,128]{2,1,0:T(8,128)S(1)}, f32[3,512,128]{2,1,0:T(8,128)}, u32[]{:S(2)}) copy-start(f32[3,512,128]{2,1,0:T(8,128)} %param.9) | copy-start | bytes 2359300
  38.2 37.1 %copy-start.4 = (s32[2304]{0:T(1024)}, s32[2304]{0:T(1024)S(1)}, u32[]{:S(2)}) copy-start(s32[2304]{0:T(1024)S(1)} %compare_select_fusion.2) | copy-start | bytes 27652
  48.0 13.9 %all-to-all-start = ((s32[8,3,114]{2,1,0:T(4,128)}), s32[8,3,114]{2,1,0:T(4,128)S(1)}, u32[]{:S(2)}, u32[]{:S(2)}) async-start(s32[8,3,114]{2,1,0:T(4,128)} %reshape.136), calls=%async_computation | async-start | bytes 32768 | tf_op jit(solution)/shard_map/all_to_all | solution.py:44
  71.5 21.4 %all-to-all-start.1 = ((bf16[8,3,114,128]{3,2,1,0:T(8,128)(2,1)}), bf16[8,3,114,128]{3,2,1,0:T(8,128)(2,1)S(1)}, u32[]{:S(2)}, u32[]{:S(2)}) async-start(bf16[8,3,114,128]{3,2,1,0:T(8,128)(2,1)} %multiply_convert_fusion), calls=%async_computation.1 | async-start | bytes 1474560 | tf_op jit(solution)/shard_map/all_to_all | solution.py:55
  75.1 61.4 %all-reduce.2.cloned.1.call-start = ((), (), s32[]{:S(2)}) async-start(), calls=%async_computation.3 | async-start | bytes 1048576 | tf_op jit(solution)/shard_map/psum | solution.py:71
  101.6 0.8 copy-start.2
  102.6 33.8 %copy-start.5 = (f32[1024]{0:T(1024)S(1)}, f32[1024]{0:T(1024)}, u32[]{:S(2)}) copy-start(f32[1024]{0:T(1024)} %param.12) | copy-start | bytes 12292
  102.6 33.8 %copy-start.6 = (f32[1024]{0:T(1024)S(1)}, f32[1024]{0:T(1024)}, u32[]{:S(2)}) copy-start(f32[1024]{0:T(1024)} %param.11) | copy-start | bytes 12292
  102.7 35.1 %copy-start.7 = (s32[128]{0:T(128)S(1)}, s32[128]{0:T(128)}, u32[]{:S(2)}) copy-start(s32[128]{0:T(128)} %param.13) | copy-start | bytes 1540
  137.8 2.0 copy-start.3
  158.3 39.6 %all-to-all-start.2 = ((f32[8,3,114,128]{3,2,1,0:T(8,128)}), f32[8,3,114,128]{3,2,1,0:T(8,128)S(1)}, u32[]{:S(2)}, u32[]{:S(2)}) async-start(f32[8,3,114,128]{3,2,1,0:T(8,128)} %reshape.142), calls=%async_computation.2 | async-start | bytes 2949120 | tf_op jit(solution)/shard_map/all_to_all | solution.py:83
Sparse Core Ops, SparseCore 0:
  104.0 32.4 all-reduce.1
where the time goes:
time: 226 us
  waiting for transfers between devices  90.3 us (40%)
  local copies, waits for them, and re-layouts  55.4 us (25%)
  other arithmetic  46 us (20%)
  starting transfers between devices  16.6 us (7%)
  between operations  14.3 us (6%)
  matrix products  3 us (1%)
    all_to_all x1, waiting for transfers between devices, body(): lax.all_to_all(outgoing_grads.reshape(row_devices, 3, unique_cap, emb_wid...  33.5 us
    psum x1, waiting for transfers between devices, body(): pre_act = lax.psum(partial_pre, 'grp') + b_first  32.6 us
    scatter-add x1, other arithmetic, body(): table_grad = jnp.zeros((3 * rows_dev, emb_width), jnp.float32).at[owner_i...  19.7 us
    all_to_all x1, waiting for transfers between devices, body(): lax.all_to_all(fetched, 'rows', split_axis=0, concat_axis=0, tiled=True)  17.6 us
    scatter-add x1, other arithmetic, body(): jnp.zeros((row_devices * 3 * unique_cap, emb_width), jnp.float32)  14.9 us
    gather x1, local copies, waits for them, and re-layouts, body(): sorted_keys = group_key[ordering]  12.3 us
    scatter x1, local copies, waits for them, and re-layouts, body(): slot_of = jnp.zeros((lookups,), jnp.int32).at[ordering].set(slot_sorted)  9 us
    scatter x1, local copies, waits for them, and re-layouts, body(): jnp.full((row_devices * 3 * unique_cap,), -1, jnp.int32).at[slot_of]  8.99 us
  transfers between devices with their start and end apart: 4, of which 4 were waited for; matrix products, arithmetic and copies ran while one was open for 0% of the time, Pallas kernels for 0%

commit v1 on v0

--- a/solution.py
+++ b/solution.py
@@ -2,6 +2,10 @@
 import jax.numpy as jnp
 from jax import lax
 from jax.sharding import PartitionSpec as P
+
+
+def render_blocks(slab_in):
+    return jnp.sum(lax.all_gather(slab_in, "grp"), axis=0)
 
 
 def head_loss(pre_act, w_out, targets):
@@ -68,7 +72,7 @@
     share_rows = bdev_rows // lax.axis_size("grp")
     share_start = lax.axis_index("grp") * share_rows
     partial_pre = jnp.dot(features, w_first, preferred_element_type=jnp.float32)
-    pre_act = lax.psum(partial_pre, "grp") + b_first
+    pre_act = render_blocks(partial_pre) + b_first
     all_losses, grad_pre = head_loss(pre_act, w_out, targets)
     losses = lax.dynamic_slice_in_dim(all_losses, share_start, share_rows, 0)
     grad_emb = jnp.dot(grad_pre, w_first.T, preferred_element_type=jnp.float32).reshape(

time: 226 us -> 218 us (0.965)
  waiting for transfers between devices: 90.3 us -> 80.6 us
    psum x1 -> x0, waiting for transfers between devices: 32.6 us -> none  [body(): pre_act = lax.psum(partial_pre, 'grp') + b_first]
    all_gather x0 -> x1, waiting for transfers between devices: none -> 21.7 us  [render_blocks(): return jnp.sum(lax.all_gather(slab_in, 'grp'), axis=0)]
where the time goes in v1:
time: 218 us; the launch traced here: 217 us
  waiting for transfers between devices  80.6 us (37%)
  local copies, waits for them, and re-layouts  56.5 us (26%)
  other arithmetic  46.6 us (21%)
  starting transfers between devices  16.6 us (8%)
  between operations  14.3 us (7%)
  matrix products  2.66 us (1%)
    all_to_all x1, waiting for transfers between devices, body(): lax.all_to_all(outgoing_grads.reshape(row_devices, 3, unique_cap, emb_wid...  34.7 us
    all_gather x1, waiting for transfers between devices, render_blocks(): return jnp.sum(lax.all_gather(slab_in, 'grp'), axis=0)  21.7 us
    scatter-add x1, other arithmetic, body(): table_grad = jnp.zeros((3 * rows_dev, emb_width), jnp.float32).at[owner_i...  19.7 us
    all_to_all x1, waiting for transfers between devices, body(): lax.all_to_all(fetched, 'rows', split_axis=0, concat_axis=0, tiled=True)  17.6 us
    scatter-add x1, other arithmetic, body(): jnp.zeros((row_devices * 3 * unique_cap, emb_width), jnp.float32)  14.9 us
    gather x1, local copies, waits for them, and re-layouts, body(): sorted_keys = group_key[ordering]  12.3 us
    scatter x1, local copies, waits for them, and re-layouts, body(): slot_of = jnp.zeros((lookups,), jnp.int32).at[ordering].set(slot_sorted)  9 us
    scatter x1, local copies, waits for them, and re-layouts, body(): jnp.full((row_devices * 3 * unique_cap,), -1, jnp.int32).at[slot_of]  8.99 us
  transfers between devices with their start and end apart: 4, of which 4 were waited for; matrix products, arithmetic and copies ran while one was open for 0% of the time, Pallas kernels for 0%

profile of v1, /device:TPU:0, one launch (start us, length us, event | category | flops | bytes accessed | tf_op | source)
XLA Modules:
  0.0 217.4 jit_solution(17948422743095148726)
XLA Ops:
  7.2 1.1 copy.27
  8.3 0.2 reshape.183
  8.5 0.7 broadcast_multiply_fusion
  9.2 0.3 copy.26
  9.4 0.2 mul.93
  9.7 5.8 %sort.17 = (s32[2304]{0:T(1024)}, s32[2304]{0:T(1024)S(1)}) sort(s32[2304]{0:T(1024)S(1)} %fusion.12, s32[2304]{0:T(1024)S(1)} %iota.15), dimensions={0}, to_apply=%region_0.1 | sort | flops 27648 | bytes 36864 | tf_op jit(solution)/shard_map/jit(argsort)/sort | solution.py:40
  15.5 12.3 %gather_fusion = s32[2304]{0:T(1024)S(1)} fusion(s32[2304]{0:T(1024)S(1)} %fusion.12, s32[3072]{0:T(1024)S(1)} %pad_clamp_fusion.2), kind=kCustom, calls=%fused_computation | custom fusion | bytes 27648 | tf_op jit(solution)/shard_map/gather | solution.py:41
  27.9 0.3 reduce-window.16
  28.3 0.1 slice_reduce_fusion.1
  28.5 0.1 fusion.19
  28.6 0.3 reduce-window.24
  29.0 0.1 slice_reduce_fusion
  29.1 0.1 bitcast_subtract_fusion
  29.2 9.0 %scatter_custom_fusion = s32[2304]{0:T(1024)S(1)} fusion(s32[2304]{0:T(1024)S(1)} %compare_select_fusion.3, s32[2304]{0:T(1024)S(1)} %bitcast_subtract_fusion, s32[]{:T(128)} %constant.33.clone.1), kind=kCustom, calls=%fused_computation.64 | custom fusion | bytes 9220 | tf_op jit(solution)/shard_map/scatter | solution.py:46
  38.2 9.0 %scatter_custom_fusion.1 = s32[2736]{0:T(1024)S(1)} fusion(s32[2304]{0:T(1024)S(1)} %compare_select_fusion.2, s32[2304]{0:T(1024)S(1)} %reshape.183, s32[]{:T(128)} %constant.31.clone.1), kind=kCustom, calls=%fused_computation.66 | custom fusion | bytes 10948 | tf_op jit(solution)/shard_map/scatter | solution.py:47
  47.3 0.7 reshape.136
  48.0 7.3 %all-to-all-start = ((s32[8,3,114]{2,1,0:T(4,128)}), s32[8,3,114]{2,1,0:T(4,128)S(1)}, u32[]{:S(2)}, u32[]{:S(2)}) async-start(s32[8,3,114]{2,1,0:T(4,128)} %reshape.136), calls=%async_computation | async-start | bytes 32768 | tf_op jit(solution)/shard_map/all_to_all | solution.py:48
  55.3 6.6 %all-to-all-done = s32[8,3,114]{2,1,0:T(4,128)S(1)} async-done(((s32[8,3,114]{2,1,0:T(4,128)}), s32[8,3,114]{2,1,0:T(4,128)S(1)}, u32[]{:S(2)}, u32[]{:S(2)}) %all-to-all-start) | async-done | bytes 10976 | tf_op jit(solution)/shard_map/all_to_all | solution.py:48
  61.8 0.1 compare_and_fusion
  61.9 0.1 reshape.137
  62.1 5.9 %gather_fusion.1 = f32[2736,128]{1,0:T(8,128)} fusion(f32[1536,128]{1,0:T(8,128)S(1)} %bitcast.20, s32[3072]{0:T(1024)S(1)} %pad_clamp_fusion.1), kind=kCustom, calls=%fused_computation.1 | custom fusion | bytes 2812608 | tf_op jit(solution)/shard_map/jit(_take)/gather | solution.py:57
  68.0 1.4 gather.14
  69.5 2.1 multiply_convert_fusion
  71.5 3.5 %all-to-all-start.1 = ((bf16[8,3,114,128]{3,2,1,0:T(8,128)(2,1)}), bf16[8,3,114,128]{3,2,1,0:T(8,128)(2,1)S(1)}, u32[]{:S(2)}, u32[]{:S(2)}) async-start(bf16[8,3,114,128]{3,2,1,0:T(8,128)(2,1)} %multiply_convert_fusion), calls=%async_computation.1 | async-start | bytes 1474560 | tf_op jit(solution)/shard_map/all_to_all | solution.py:59
  75.1 0.2 all-gather.3.cloned.1.call-start
  75.3 17.6 %all-to-all-done.1 = bf16[8,3,114,128]{3,2,1,0:T(8,128)(2,1)S(1)} async-done(((bf16[8,3,114,128]{3,2,1,0:T(8,128)(2,1)}), bf16[8,3,114,128]{3,2,1,0:T(8,128)(2,1)S(1)}, u32[]{:S(2)}, u32[]{:S(2)}) %all-to-all-start.1) | async-done | bytes 700448 | tf_op jit(solution)/shard_map/all_to_all | solution.py:59
  93.0 0.2 reshape.139
  93.2 5.6 %gather_fusion.2 = bf16[2304,128]{1,0:T(8,128)(2,1)} fusion(bf16[2736,128]{1,0:T(8,128)(2,1)S(1)} %reshape.139, s32[3072]{0:T(1024)S(1)} %pad_clamp_fusion), kind=kCustom, calls=%fused_computation.2 | custom fusion | bytes 1188864 | tf_op jit(solution)/shard_map/gather | solution.py:65
  98.8 2.0 reshape.146
  100.8 0.8 fusion.27
  101.6 0.8 copy-done.2
  102.4 0.1 fusion.2
  102.5 0.2 copy.31
  102.6 1.2 fusion.28
  103.9 21.7 %all-gather.3.cloned.1.call-done = f32[512,1024]{1,0:T(8,128)} async-done(((f32[128,1024]{1,0:T(8,128)}), f32[512,1024]{1,0:T(8,128)}) %all-gather.3.cloned.1.call-update) | async-done | bytes 2097168 | tf_op jit(solution)/shard_map/all_gather | solution.py:8
  125.6 1.8 reduce_sum.18
  127.4 0.2 multiply_reduce_fusion
  127.7 1.5 fusion.5
  129.1 1.2 copy.33
  130.5 0.8 copy.36
  131.3 1.4 reshape.191
  132.7 14.9 %scatter_custom_fusion.2 = f32[2736,128]{1,0:T(8,128)S(1)} fusion(s32[2304]{0:T(1024)} %copy-done.4, f32[2304,128]{1,0:T(8,128)} %reshape.191, f32[]{:T(128)} %constant.26.clone.1), kind=kCustom, calls=%fused_computation.9 | custom fusion | flops 294912 | bytes 1401344 | tf_op jit(solution)/shard_map/scatter-add | solution.py:85
  147.6 1.2 reshape.142
  148.8 5.5 %all-to-all-start.2 = ((f32[8,3,114,128]{3,2,1,0:T(8,128)}), f32[8,3,114,128]{3,2,1,0:T(8,128)S(1)}, u32[]{:S(2)}, u32[]{:S(2)}) async-start(f32[8,3,114,128]{3,2,1,0:T(8,128)} %reshape.142), calls=%async_computation.2 | async-start | bytes 2949120 | tf_op jit(solution)/shard_map/all_to_all | solution.py:87
  154.3 0.6 dynamic_slice.3
  154.9 34.7 %all-to-all-done.2 = f32[8,3,114,128]{3,2,1,0:T(8,128)S(1)} async-done(((f32[8,3,114,128]{3,2,1,0:T(8,128)}), f32[8,3,114,128]{3,2,1,0:T(8,128)S(1)}, u32[]{:S(2)}, u32[]{:S(2)}) %all-to-all-start.2) | async-done | bytes 1400864 | tf_op jit(solution)/shard_map/all_to_all | solution.py:87
  189.6 1.2 reshape.199
  190.8 19.7 %scatter_custom_fusion.3 = f32[1536,128]{1,0:T(8,128)} fusion(s32[2736]{0:T(1024)S(1)} %fusion.20, f32[2736,128]{1,0:T(8,128)} %reshape.199, f32[]{:T(128)} %constant.26.clone.1), kind=kCustom, calls=%fused_computation.16 | custom fusion | flops 350208 | bytes 786944 | tf_op jit(solution)/shard_map/scatter-add | solution.py:97
  (36 shorter events, 0.8 us)
Async XLA Ops:
  7.2 95.5 %copy-start = (bf16[768,1024]{1,0:T(8,128)(2,1)S(1)}, bf16[768,1024]{1,0:T(8,128)(2,1)}, u32[]{:S(2)}) copy-start(bf16[768,1024]{1,0:T(8,128)(2,1)} %param.10) | copy-start | bytes 4718596
  15.4 46.7 %copy-start.1 = (f32[3,512,128]{2,1,0:T(8,128)S(1)}, f32[3,512,128]{2,1,0:T(8,128)}, u32[]{:S(2)}) copy-start(f32[3,512,128]{2,1,0:T(8,128)} %param.9) | copy-start | bytes 2359300
  38.2 37.1 %copy-start.4 = (s32[2304]{0:T(1024)}, s32[2304]{0:T(1024)S(1)}, u32[]{:S(2)}) copy-start(s32[2304]{0:T(1024)S(1)} %compare_select_fusion.2) | copy-start | bytes 27652
  48.0 13.9 %all-to-all-start = ((s32[8,3,114]{2,1,0:T(4,128)}), s32[8,3,114]{2,1,0:T(4,128)S(1)}, u32[]{:S(2)}, u32[]{:S(2)}) async-start(s32[8,3,114]{2,1,0:T(4,128)} %reshape.136), calls=%async_computation | async-start | bytes 32768 | tf_op jit(solution)/shard_map/all_to_all | solution.py:48
  71.5 21.4 %all-to-all-start.1 = ((bf16[8,3,114,128]{3,2,1,0:T(8,128)(2,1)}), bf16[8,3,114,128]{3,2,1,0:T(8,128)(2,1)S(1)}, u32[]{:S(2)}, u32[]{:S(2)}) async-start(bf16[8,3,114,128]{3,2,1,0:T(8,128)(2,1)} %multiply_convert_fusion), calls=%async_computation.1 | async-start | bytes 1474560 | tf_op jit(solution)/shard_map/all_to_all | solution.py:59
  75.1 50.5 %all-gather.3.cloned.1.call-start = ((), (), s32[]{:S(2)}) async-start(), calls=%async_computation.3 | async-start | bytes 2621440 | tf_op jit(solution)/shard_map/all_gather | solution.py:8
  101.6 0.8 copy-start.2
  103.9 23.5 %copy-start.5 = (f32[1024]{0:T(1024)S(1)}, f32[1024]{0:T(1024)}, u32[]{:S(2)}) copy-start(f32[1024]{0:T(1024)} %param.12) | copy-start | bytes 12292
  103.9 23.5 %copy-start.6 = (f32[1024]{0:T(1024)S(1)}, f32[1024]{0:T(1024)}, u32[]{:S(2)}) copy-start(f32[1024]{0:T(1024)} %param.11) | copy-start | bytes 12292
  125.6 2.1 copy-start.7
  127.7 2.6 %copy-start.3 = (f32[128,6,1,128]{3,2,1,0:T(1,128)S(1)}, f32[128,6,1,128]{3,2,1,0:T(1,128)}, u32[]{:S(2)}) copy-start(f32[128,6,1,128]{3,2,1,0:T(1,128)} %copy-done.2) | copy-start | bytes 1179652
  148.8 40.8 %all-to-all-start.2 = ((f32[8,3,114,128]{3,2,1,0:T(8,128)}), f32[8,3,114,128]{3,2,1,0:T(8,128)S(1)}, u32[]{:S(2)}, u32[]{:S(2)}) async-start(f32[8,3,114,128]{3,2,1,0:T(8,128)} %reshape.142), calls=%async_computation.2 | async-start | bytes 2949120 | tf_op jit(solution)/shard_map/all_to_all | solution.py:87
Sparse Core Ops, SparseCore 0:
  104.0 21.5 all-gather.2
